TPU v7x, 32 devices: a 4x4x1 block of a 4x4x8 slice. The times are simulated.
32 devices in a mesh: pod: 1 (over z), data: 4 (over y), expert: 8 (over x, core).
Axes of the slice: x: 4, y: 4, z: 1, core: 2. Of those that a mesh axis runs over, the one named last changes fastest.
The devices are a block of a 4x4x8 slice.
Arguments:
- tokens: bfloat16 [131072, 768], P(('pod', 'data', 'expert'))
- routes: int32 [131072, 1], P(('pod', 'data', 'expert'))
- gates: float32 [131072, 1], P(('pod', 'data', 'expert'))
- grad_y: bfloat16 [131072, 768], P(('pod', 'data', 'expert'))
- w_in1: bfloat16 [8, 768, 3072], P('expert')
- w_in3: bfloat16 [8, 768, 3072], P('expert')
- w_out: bfloat16 [8, 3072, 768], P('expert')
Outputs:
- output 1: bfloat16 [131072, 768], P(('pod', 'data', 'expert'))
- output 2: bfloat16 [131072, 768], P(('pod', 'data', 'expert'))
- output 3: float32 [8, 768, 3072], P(('pod', 'expert'))
- output 4: float32 [8, 768, 3072], P(('pod', 'expert'))
- output 5: float32 [8, 3072, 768], P(('pod', 'expert'))
All inputs are finite; a program needn't handle non-finite values.
Results may differ from a plain program's by a relative error of at most 0.001.
Values are sent between devices in bfloat16 or wider.
A program may use at most 768 MiB of HBM per device.

v0:
```python
import jax
import jax.numpy as jnp
from jax import lax
from jax.sharding import PartitionSpec as P

N_HOT = 2


def value_a10(tok_dev, top_k, n_exp):
    cap_hot = 3 * tok_dev // 8
    cap_cold = max(8, ((tok_dev * top_k - N_HOT * cap_hot) // (n_exp - N_HOT) + 7) // 8 * 8)
    return cap_cold, cap_hot


def route_rows(routes_dev, n_exp, cap_cold, cap_hot):
    flat_exp = routes_dev.reshape(-1)
    n_slots = flat_exp.shape[0]
    order = jnp.argsort(flat_exp, stable=True)
    counts = jax.ops.segment_sum(jnp.ones((n_slots,), jnp.int32), flat_exp, num_segments=n_exp)
    starts = jnp.cumsum(counts) - counts
    rank_sorted = jnp.arange(n_slots, dtype=jnp.int32) - starts[flat_exp[order]]
    slot_rank = jnp.zeros((n_slots,), jnp.int32).at[order].set(rank_sorted)
    hot_index = jnp.where(flat_exp == 0, 0, jnp.where(flat_exp == n_exp // 2, 1, -1))
    cold_row = jnp.where((hot_index < 0) & (slot_rank < cap_cold), flat_exp * cap_cold + slot_rank, n_exp * cap_cold)
    hot_row = jnp.where(hot_index >= 0, hot_index * cap_hot + slot_rank, N_HOT * cap_hot)
    return cold_row, hot_row


def gather_rows(slot_rows, x_local, dy_local, gate_flat, n_rows):
    n_slots = slot_rows.shape[0]
    tok_n = x_local.shape[0]
    top_k = n_slots // tok_n
    src_tok = jnp.full((n_rows,), tok_n, jnp.int32).at[slot_rows].set(
        jnp.arange(n_slots, dtype=jnp.int32) // top_k, mode='drop')
    src_gate = jnp.zeros((n_rows,), jnp.float32).at[slot_rows].set(gate_flat, mode='drop')
    x_rows = jnp.take(x_local, src_tok, axis=0, mode='fill', fill_value=0)
    dy_rows = jnp.take(dy_local, src_tok, axis=0, mode='fill', fill_value=0)
    do_rows = (dy_rows.astype(jnp.float32) * src_gate[:, None]).astype(jnp.bfloat16)
    return x_rows, do_rows


def expert_fwd(x_rows, w_a, w_b, w_c):
    pre_a = jnp.einsum('esd,edf->esf', x_rows, w_a, preferred_element_type=jnp.float32).astype(jnp.bfloat16)
    pre_b = jnp.einsum('esd,edf->esf', x_rows, w_b, preferred_element_type=jnp.float32).astype(jnp.bfloat16)
    act_a = pre_a.astype(jnp.float32)
    hidden = (act_a * jax.nn.sigmoid(act_a) * pre_b.astype(jnp.float32)).astype(jnp.bfloat16)
    outs = jnp.einsum('esf,efd->esd', hidden, w_c, preferred_element_type=jnp.float32).astype(jnp.bfloat16)
    return outs, pre_a, pre_b, hidden


def expert_bwd(x_rows, do_rows, pre_a, pre_b, hidden, w_a, w_b, w_c):
    d_hidden = jnp.einsum('esd,efd->esf', do_rows, w_c, preferred_element_type=jnp.float32)
    act_a = pre_a.astype(jnp.float32)
    act_b = pre_b.astype(jnp.float32)
    sigma_a = jax.nn.sigmoid(act_a)
    d_pre_b = (d_hidden * act_a * sigma_a).astype(jnp.bfloat16)
    d_pre_a = (d_hidden * act_b * sigma_a * (1.0 + act_a * (1.0 - sigma_a))).astype(jnp.bfloat16)
    d_rows = (jnp.einsum('esf,edf->esd', d_pre_a, w_a, preferred_element_type=jnp.float32)
              + jnp.einsum('esf,edf->esd', d_pre_b, w_b, preferred_element_type=jnp.float32)).astype(jnp.bfloat16)
    grad_a = jnp.einsum('esd,esf->edf', x_rows, d_pre_a, preferred_element_type=jnp.float32)
    grad_b = jnp.einsum('esd,esf->edf', x_rows, d_pre_b, preferred_element_type=jnp.float32)
    grad_c = jnp.einsum('esf,esd->efd', hidden, do_rows, preferred_element_type=jnp.float32)
    return d_rows, grad_a, grad_b, grad_c


def combine(cold_rows, hot_rows, cold_vals, hot_vals, weights, tok_n):
    slot_vals = (jnp.take(cold_vals, cold_rows, axis=0, mode='fill', fill_value=0)
                 + jnp.take(hot_vals, hot_rows, axis=0, mode='fill', fill_value=0))
    slot_vals = slot_vals.reshape(tok_n, -1, cold_vals.shape[1]).astype(jnp.float32)
    if weights is not None:
        slot_vals = slot_vals * weights[:, :, None]
    return jnp.sum(slot_vals, axis=1).astype(jnp.bfloat16)


def solution(mesh):
    n_dev = mesh.shape['expert']
    row_spec = P(('pod', 'data', 'expert'), None)
    w_spec = P('expert', None, None)
    grad_spec = P(('pod', 'expert'), None, None)

    def body(tokens, routes, gates, grad_y, w_in1, w_in3, w_out):
        tok_n, d_model = tokens.shape
        top_k = routes.shape[1]
        exp_local = w_in1.shape[0]
        n_exp = exp_local * n_dev
        my_index = lax.axis_index('expert')
        cap_cold, cap_hot = value_a10(tok_n, top_k, n_exp)
        cold_rows, hot_rows = route_rows(routes, n_exp, cap_cold, cap_hot)
        gate_flat = gates.reshape(-1)
        cold_x, cold_do = gather_rows(cold_rows, tokens, grad_y, gate_flat, n_exp * cap_cold)
        hot_x, hot_do = gather_rows(hot_rows, tokens, grad_y, gate_flat, N_HOT * cap_hot)
        hot_x = hot_x.reshape(N_HOT, cap_hot, d_model)
        hot_do = hot_do.reshape(N_HOT, cap_hot, d_model)
        hot_local = [0, (n_exp // 2) % exp_local]
        hot_owner = [0, (n_exp // 2) // exp_local]

        def owned_copy(w_local):
            return jnp.stack([jnp.where(my_index == owner_idx, w_local[local_idx], 0)
                              for local_idx, owner_idx in zip(hot_local, hot_owner)])

        hot_w1, hot_w3, hot_w2 = lax.psum((owned_copy(w_in1), owned_copy(w_in3), owned_copy(w_out)), 'expert')

        recv_x = lax.all_to_all(cold_x.reshape(n_exp, cap_cold, d_model), 'expert', 0, 1, tiled=True)
        cold_out, cold_pre_a, cold_pre_b, cold_hidden = expert_fwd(recv_x, w_in1, w_in3, w_out)
        back_out = lax.all_to_all(cold_out, 'expert', 1, 0, tiled=True)
        hot_out, hot_pre_a, hot_pre_b, hot_hidden = expert_fwd(hot_x, hot_w1, hot_w3, hot_w2)
        y_out = combine(cold_rows, hot_rows, back_out.reshape(-1, d_model), hot_out.reshape(-1, d_model), gates, tok_n)

        recv_do = lax.all_to_all(cold_do.reshape(n_exp, cap_cold, d_model), 'expert', 0, 1, tiled=True)
        cold_dx, grad_w1, grad_w3, grad_w2 = expert_bwd(recv_x, recv_do, cold_pre_a, cold_pre_b, cold_hidden, w_in1, w_in3, w_out)
        back_dx = lax.all_to_all(cold_dx, 'expert', 1, 0, tiled=True)
        hot_dx, part_w1, part_w3, part_w2 = expert_bwd(hot_x, hot_do, hot_pre_a, hot_pre_b, hot_hidden, hot_w1, hot_w3, hot_w2)
        grad_x = combine(cold_rows, hot_rows, back_dx.reshape(-1, d_model), hot_dx.reshape(-1, d_model), None, tok_n)
        part_w1, part_w3, part_w2 = lax.psum((part_w1, part_w3, part_w2), 'expert')

        def add_owned(grad_local, hot_sum):
            for slot_h in range(N_HOT):
                grad_local = grad_local.at[hot_local[slot_h]].add(
                    jnp.where(my_index == hot_owner[slot_h], hot_sum[slot_h], 0.0))
            return grad_local

        grad_w1 = add_owned(grad_w1, part_w1)
        grad_w3 = add_owned(grad_w3, part_w3)
        grad_w2 = add_owned(grad_w2, part_w2)
        grad_w1, grad_w3, grad_w2 = lax.psum((grad_w1, grad_w3, grad_w2), 'data')
        return y_out, grad_x, grad_w1, grad_w3, grad_w2

    return jax.shard_map(body, mesh=mesh,
                         in_specs=(row_spec, row_spec, row_spec, row_spec, w_spec, w_spec, w_spec),
                         out_specs=(row_spec, row_spec, grad_spec, grad_spec, grad_spec),
                         check_vma=False)
```

profile of v0, /device:TPU:97, one launch (start us, length us, event | category | flops | bytes accessed | tf_op | source)
XLA Modules:
  0.0 1643.9 jit_solution(5925529390829583078)
XLA Ops:
  7.3 6.7 broadcast_select_fusion.2
  13.9 8.4 pad_maximum_fusion.2
  22.3 9.3 broadcast_select_fusion.5
  31.6 8.4 pad_maximum_fusion.1
  40.0 8.4 pad_maximum_fusion
  49.1 28.8 %scatter_custom_fusion = s32[8]{0:T(128)S(1)} fusion(s32[4096]{0:T(1024)S(1)} %bitcast.143, s32[4096]{0:T(1024)S(1)} %broadcast_in_dim.108, s32[]{:T(128)} %constant.197.clone.1), kind=kCustom, calls=%fused_computation.146 | custom fusion | flops 4096 | bytes 36 | tf_op jit(solution)/shard_map/scatter-add | solution.py:19
  78.1 5.8 sort.17
  83.8 23.0 %gather_fusion = s32[4096]{0:T(1024)S(1)} fusion(s32[4096]{0:T(1024)S(1)} %bitcast.145, s32[4096]{0:T(1024)S(1)} %get-tuple-element.110), kind=kCustom, calls=%fused_computation.8 | custom fusion | bytes 49152 | tf_op jit(solution)/shard_map/gather | solution.py:21
  107.6 4.5 compare_select_fusion.1
  112.8 15.5 scatter_custom_fusion.1
  129.0 16.0 scatter_custom_fusion.3
  145.0 18.2 %gather_fusion.7 = bf16[3072,768]{1,0:T(8,128)(2,1)} fusion(bf16[4096,768]{1,0:T(8,128)(2,1)} %param.30, s32[3072]{0:T(1024)S(1)} %fusion.59), kind=kCustom, calls=%fused_computation.6.clone | custom fusion | bytes 9449472 | tf_op jit(solution)/shard_map/jit(_take)/gather | solution.py:37
  163.2 18.2 %gather_fusion.3 = bf16[3072,768]{1,0:T(8,128)(2,1)} fusion(bf16[4096,768]{1,0:T(8,128)(2,1)} %param.27, s32[3072]{0:T(1024)S(1)} %fusion.59), kind=kCustom, calls=%fused_computation.2.clone | custom fusion | bytes 9449472 | tf_op jit(solution)/shard_map/jit(_take)/gather | solution.py:36
  181.3 15.7 scatter_custom_fusion.5
  197.1 5.6 broadcast_select_fusion
  202.6 6.1 multiply_convert_fusion.1
  208.7 129.8 %all-reduce.11.cloned.1.call-done = (bf16[2,768,3072]{2,1,0:T(8,128)(2,1)}, bf16[2,768,3072]{2,1,0:T(8,128)(2,1)}, bf16[2,3072,768]{2,1,0:T(8,128)(2,1)}) async-done(((bf16[2,768,3072]{2,1,0:T(8,128)(2,1)}, bf16[2,768,3072]{2,1,0:T(8,128)(2,1)}, bf16[2,3072,768]{2,1,0:T(8,128)(2,1)}), (bf16[2,768,3072]{2,1,0:T(8,128)(2,1)}, bf16[2,768,3072]{2,1,0:T(8,128)(2,1)}, ...) | async-done | bytes 28311568 | tf_op jit(solution)/shard_map/psum | solution.py:101
  338.5 22.1 %convolution_convert_fusion = bf16[2,1536,3072]{2,1,0:T(8,128)(2,1)} fusion(bf16[2,1536,768]{2,1,0:T(8,128)(2,1)} %bitcast.151, bf16[2,768,3072]{2,1,0:T(8,128)(2,1)} %get-tuple-element.89), kind=kOutput, calls=%fused_computation.47 | convolution fusion | flops 14504951808 | bytes 33030144 | tf_op jit(solution)/shard_map/esd,edf->esf/dot_general | solution.py:44
  360.6 21.2 %convolution_convert_fusion.1 = bf16[2,1536,3072]{2,1,0:T(8,128)(2,1)} fusion(bf16[2,1536,768]{2,1,0:T(8,128)(2,1)S(1)} %bitcast.155, bf16[2,768,3072]{2,1,0:T(8,128)(2,1)} %get-tuple-element.90), kind=kOutput, calls=%fused_computation.48 | convolution fusion | flops 14504951808 | bytes 33030144 | tf_op jit(solution)/shard_map/esd,edf->esf/dot_general | solution.py:43
  381.9 44.6 %fusion.9 = (bf16[2,1536,3072]{2,1,0:T(8,128)(2,1)}, bf16[2,1536,3072]{2,1,0:T(8,128)(2,1)}, bf16[2,1536,3072]{2,1,0:T(8,128)(2,1)}) fusion(bf16[2,1536,3072]{2,1,0:T(8,128)(2,1)} %convolution_convert_fusion.1, bf16[2,1536,3072]{2,1,0:T(8,128)(2,1)} %convolution_convert_fusion, bf16[2,1536,768]{2,1,0:T(8,128)(2,1)} %bitcast.165, ...), kind=kOutput, calls=%fused_computation.30 | convolution fusion | flops 14665383936 | bytes 108527616 | tf_op jit(solution)/shard_map/esd,efd->esf/dot_general | solution.py:52
  426.5 22.5 %fusion.75 = f32[2,768,3072]{2,1,0:T(8,128)} fusion(bf16[2,1536,768]{2,1,0:T(8,128)(2,1)} %bitcast.152, bf16[2,1536,3072]{2,1,0:T(8,128)(2,1)} %get-tuple-element.96), kind=kOutput, calls=%fused_computation.153 | convolution fusion | flops 14495514624 | bytes 42467328 | tf_op jit(solution)/shard_map/esd,esf->edf/dot_general | solution.py:61
  449.0 21.6 %fusion.74 = f32[2,768,3072]{2,1,0:T(8,128)} fusion(bf16[2,1536,768]{2,1,0:T(8,128)(2,1)S(1)} %bitcast.156, bf16[2,1536,3072]{2,1,0:T(8,128)(2,1)} %get-tuple-element.97), kind=kOutput, calls=%fused_computation.152 | convolution fusion | flops 14495514624 | bytes 42467328 | tf_op jit(solution)/shard_map/esd,esf->edf/dot_general | solution.py:60
  470.7 21.9 %fusion.76 = f32[2,3072,768]{2,1,0:T(8,128)} fusion(bf16[2,1536,3072]{2,1,0:T(8,128)(2,1)} %get-tuple-element.98, bf16[2,1536,768]{2,1,0:T(8,128)(2,1)S(1)} %bitcast.168), kind=kOutput, calls=%fused_computation.154 | convolution fusion | flops 14495514624 | bytes 42467328 | tf_op jit(solution)/shard_map/esf,esd->efd/dot_general | solution.py:62
  492.7 15.8 scatter_custom_fusion.2
  508.5 10.1 gather_fusion.1
  520.2 5.1 all-to-all-start
  525.3 15.6 scatter_custom_fusion.4
  541.0 10.1 gather_fusion.5
  553.0 11.0 all-to-all-done
  564.1 4.5 all-to-all-start.2
  568.6 11.6 convolution_convert_fusion.2
  580.2 10.8 convolution_convert_fusion.3
  591.0 16.2 all-to-all-done.2
  607.2 21.6 %fusion.13 = (bf16[1408,3072]{1,0:T(8,128)(2,1)}, bf16[1408,3072]{1,0:T(8,128)(2,1)}, bf16[1408,3072]{1,0:T(8,128)(2,1)}) fusion(bf16[1408,3072]{1,0:T(8,128)(2,1)} %convolution_convert_fusion.2, bf16[1408,3072]{1,0:T(8,128)(2,1)} %convolution_convert_fusion.3, bf16[1408,768]{1,0:T(8,128)(2,1)S(1)} %bitcast.171, bf16[1,3072,768]{2,1,0:T(8,128)(2,1)} %param.33), kind=kOutput, calls=%fused_computation.40 | convolution fusion | flops 6721634304 | bytes 50135040 | tf_op jit(solution)/shard_map/esd,efd->esf/dot_general | solution.py:52
  628.8 461.9 %all-reduce.7.cloned.1.call-done = (f32[2,768,3072]{2,1,0:T(8,128)}, f32[2,768,3072]{2,1,0:T(8,128)}, f32[2,3072,768]{2,1,0:T(8,128)}) async-done(((f32[2,768,3072]{2,1,0:T(8,128)}, f32[2,768,3072]{2,1,0:T(8,128)}, f32[2,3072,768]{2,1,0:T(8,128)}), (f32[2,768,3072]{2,1,0:T(8,128)}, f32[2,768,3072]{2,1,0:T(8,128)}, f32[2,3072,768]{2,1,0:T(8,128)})) %all-reduce.7.cloned.1.call-update) | async-done | bytes 56623120 | tf_op jit(solution)/shard_map/psum | solution.py:114
  1090.7 17.7 %fusion.22 = f32[1,3072,768]{2,1,0:T(8,128)} fusion(f32[2,3072,768]{2,1,0:T(8,128)} %get-tuple-element.85, bf16[1408,3072]{1,0:T(8,128)(2,1)} %get-tuple-element.101, bf16[1408,768]{1,0:T(8,128)(2,1)S(1)} %bitcast.172, pred[]{:T(512)S(6)} %eq.14, pred[]{:T(512)S(6)} %eq.13), kind=kOutput, calls=%fused_computation.55 | convolution fusion | flops 6653214720 | bytes 39124992 | tf_op jit(solution)/shard_map/esf,esd->efd/dot_general | solution.py:62
  1108.4 15.6 fusion.32
  1124.0 17.5 %fusion.27 = f32[1,768,3072]{2,1,0:T(8,128)} fusion(f32[2,768,3072]{2,1,0:T(8,128)} %get-tuple-element.84, bf16[1408,768]{1,0:T(8,128)(2,1)} %bitcast.14, bf16[1408,3072]{1,0:T(8,128)(2,1)} %get-tuple-element.100, pred[]{:T(512)S(6)} %eq.14, pred[]{:T(512)S(6)} %eq.13), kind=kOutput, calls=%fused_computation.62 | convolution fusion | flops 6653214720 | bytes 39124992 | tf_op jit(solution)/shard_map/esd,esf->edf/dot_general | solution.py:61
  1141.5 10.7 fusion.53
  1152.3 16.4 copy.40
  1169.3 13.7 reduce.14
  1186.2 4.4 all-to-all-start.1
  1190.6 10.8 fusion.39
  1201.3 10.8 fusion.50
  1212.2 16.4 copy.39
  1228.6 14.9 reduce.15
  1243.5 5.8 reshape.622
  1249.3 5.2 all-to-all-start.3
  1254.6 4.4 reshape.621
  1261.5 19.7 %all-to-all-done.3 = bf16[8,2,67584]{2,1,0:T(2,128)(2,1)} async-done(((bf16[8,2,67584]{2,1,0:T(2,128)(2,1)}), bf16[8,2,67584]{2,1,0:T(2,128)(2,1)}, u32[]{:S(2)}, u32[]{:S(2)}) %all-to-all-start.3) | async-done | bytes 2162720 | tf_op jit(solution)/shard_map/all_to_all | solution.py:111
  1281.2 6.8 reshape.623
  1288.0 3.9 copy.37
  1291.9 17.8 %gather_fusion.2 = bf16[4096,768]{1,0:T(8,128)(2,1)} fusion(bf16[1408,768]{1,0:T(8,128)(2,1)S(1)} %bitcast.147, s32[4096]{0:T(1024)S(1)} %get-tuple-element.121), kind=kCustom, calls=%fused_computation.1.clone | custom fusion | bytes 12599296 | tf_op jit(solution)/shard_map/jit(_take)/gather | solution.py:67
  1309.7 21.0 %gather_fusion.6 = bf16[4096,768]{1,0:T(8,128)(2,1)} fusion(bf16[1408,768]{1,0:T(8,128)(2,1)} %bitcast.148, s32[4096]{0:T(1024)S(1)} %get-tuple-element.121), kind=kCustom, calls=%fused_computation.5.clone | custom fusion | bytes 12599296 | tf_op jit(solution)/shard_map/jit(_take)/gather | solution.py:67
  1330.8 21.8 %convolution_convert_fusion.4 = bf16[2,1536,768]{2,1,0:T(8,128)(2,1)} fusion(bf16[2,1536,3072]{2,1,0:T(8,128)(2,1)} %get-tuple-element.98, bf16[2,3072,768]{2,1,0:T(8,128)(2,1)} %get-tuple-element.91), kind=kOutput, calls=%fused_computation.97 | convolution fusion | flops 14497873920 | bytes 33030144 | tf_op jit(solution)/shard_map/esf,efd->esd/dot_general | solution.py:47
  1352.5 22.0 %gather_fusion.4 = bf16[4096,768]{1,0:T(8,128)(2,1)} fusion(bf16[3072,768]{1,0:T(8,128)(2,1)} %bitcast.150, s32[4096]{0:T(1024)S(1)} %get-tuple-element.120), kind=kCustom, calls=%fused_computation.3.clone | custom fusion | bytes 12599296 | tf_op jit(solution)/shard_map/jit(_take)/gather | solution.py:68
  1374.5 22.4 %fusion.73 = f32[2,1536,768]{2,1,0:T(8,128)} fusion(bf16[2,1536,3072]{2,1,0:T(8,128)(2,1)} %get-tuple-element.97, bf16[2,768,3072]{2,1,0:T(8,128)(2,1)} %get-tuple-element.90), kind=kOutput, calls=%fused_computation.151 | convolution fusion | flops 14495514624 | bytes 37748736 | tf_op jit(solution)/shard_map/esf,edf->esd/dot_general | solution.py:58
  1396.9 23.0 %add_convert_fusion = bf16[2,1536,768]{2,1,0:T(8,128)(2,1)} fusion(f32[2,1536,768]{2,1,0:T(8,128)} %fusion.73, bf16[2,1536,3072]{2,1,0:T(8,128)(2,1)} %get-tuple-element.96, bf16[2,768,3072]{2,1,0:T(8,128)(2,1)} %get-tuple-element.89), kind=kOutput, calls=%fused_computation.76 | convolution fusion | flops 14500233216 | bytes 42467328 | tf_op jit(solution)/shard_map/esf,edf->esd/dot_general | solution.py:59
  1420.0 22.0 %gather_fusion.8 = bf16[4096,768]{1,0:T(8,128)(2,1)} fusion(bf16[3072,768]{1,0:T(8,128)(2,1)} %bitcast.149, s32[4096]{0:T(1024)S(1)} %get-tuple-element.120), kind=kCustom, calls=%fused_computation.7.clone | custom fusion | bytes 12599296 | tf_op jit(solution)/shard_map/jit(_take)/gather | solution.py:68
  1442.0 10.0 select_add_fusion
  1452.0 8.3 multiply_convert_fusion
  1460.2 156.9 %all-reduce.9.cloned.1.call-done = (f32[1,768,3072]{2,1,0:T(8,128)}, f32[1,768,3072]{2,1,0:T(8,128)}, f32[1,3072,768]{2,1,0:T(8,128)}) async-done(((f32[1,768,3072]{2,1,0:T(8,128)}, f32[1,768,3072]{2,1,0:T(8,128)}, f32[1,3072,768]{2,1,0:T(8,128)}), (f32[1,768,3072]{2,1,0:T(8,128)}, f32[1,768,3072]{2,1,0:T(8,128)}, f32[1,3072,768]{2,1,0:T(8,128)})) %all-reduce.9.cloned.1.call-update) | async-done | bytes 28311568 | tf_op jit(solution)/shard_map/psum | solution.py:125
  1617.2 9.8 copy.50
  1627.0 4.8 copy.51
  (74 shorter events, 18.4 us)
Async XLA Ops:
  7.2 331.3 %all-reduce.11.cloned.1.call-start = ((), (), s32[]{:S(2)}) async-start(), calls=%async_computation.6 | async-start | bytes 56623104 | tf_op jit(solution)/shard_map/psum | solution.py:101
  48.4 0.7 copy-start
  48.4 1042.2 %all-reduce.7.cloned.1.call-start = ((), (), s32[]{:S(2)}) async-start(), calls=%async_computation.4 | async-start | bytes 113246208 | tf_op jit(solution)/shard_map/psum | solution.py:114
  129.0 52.3 %copy-start.5 = (s32[4096]{0:T(1024)}, s32[4096]{0:T(1024)S(1)}, u32[]{:S(2)}) copy-start(s32[4096]{0:T(1024)S(1)} %get-tuple-element.109) | copy-start | bytes 49156
  202.6 158.0 %slice-start = ((s8[4718592]{0:T(1024)(128)(4,1)}), s8[524288]{0:T(1024)(128)(4,1)S(1)}, s32[]{:S(2)}) async-start(s8[4718592]{0:T(1024)(128)(4,1)} %bitcast.153), calls=%async_computation.7 | async-start | bytes 1048576
  338.5 22.1 %slice-start.1 = ((s8[4718592]{0:T(1024)(128)(4,1)}), s8[4194304]{0:T(1024)(128)(4,1)S(1)}, s32[]{:S(2)}) async-start(s8[4718592]{0:T(1024)(128)(4,1)} %bitcast.153), calls=%async_computation.8 | async-start | bytes 8388608
  426.5 22.5 %copy-start.1 = (bf16[3072,768]{1,0:T(8,128)(2,1)S(1)}, bf16[3072,768]{1,0:T(8,128)(2,1)}, u32[]{:S(2)}) copy-start(bf16[3072,768]{1,0:T(8,128)(2,1)} %broadcast_select_fusion) | copy-start | bytes 14155780
  426.5 44.2 %slice-start.5 = ((s8[4718592]{0:T(1024)(128)(4,1)}), s8[4194304]{0:T(1024)(128)(4,1)S(1)}, s32[]{:S(2)}) async-start(s8[4718592]{0:T(1024)(128)(4,1)} %bitcast.166), calls=%async_computation.12 | async-start | bytes 8388608
  449.0 21.6 %slice-start.6 = ((s8[4718592]{0:T(1024)(128)(4,1)}), s8[524288]{0:T(1024)(128)(4,1)S(1)}, s32[]{:S(2)}) async-start(s8[4718592]{0:T(1024)(128)(4,1)} %bitcast.166), calls=%async_computation.13 | async-start | bytes 1048576
  520.2 43.8 %all-to-all-start = ((bf16[8,176,768]{2,1,0:T(8,128)(2,1)}), bf16[8,176,768]{2,1,0:T(8,128)(2,1)}, u32[]{:S(2)}, u32[]{:S(2)}) async-start(bf16[8,176,768]{2,1,0:T(8,128)(2,1)} %bitcast.164), calls=%async_computation | async-start | bytes 4325376 | tf_op jit(solution)/shard_map/all_to_all | solution.py:103
  564.1 16.1 slice-start.7
  564.1 43.2 %all-to-all-start.2 = ((bf16[8,176,768]{2,1,0:T(8,128)(2,1)}), bf16[8,176,768]{2,1,0:T(8,128)(2,1)S(1)}, u32[]{:S(2)}, u32[]{:S(2)}) async-start(bf16[8,176,768]{2,1,0:T(8,128)(2,1)} %bitcast.163), calls=%async_computation.2 | async-start | bytes 4325376 | tf_op jit(solution)/shard_map/all_to_all | solution.py:109
  568.6 1048.6 %all-reduce.9.cloned.1.call-start = ((), (), s32[]{:S(2)}) async-start(), calls=%async_computation.5 | async-start | bytes 56623104 | tf_op jit(solution)/shard_map/psum | solution.py:125
  568.6 11.6 slice-start.8
  1090.7 17.7 %copy-start.10 = (bf16[1408,3072]{1,0:T(8,128)(2,1)S(1)}, bf16[1408,3072]{1,0:T(8,128)(2,1)}, u32[]{:S(2)}) copy-start(bf16[1408,3072]{1,0:T(8,128)(2,1)} %get-tuple-element.99) | copy-start | bytes 25952260
  1186.2 63.1 %all-to-all-start.1 = ((bf16[8,2,67584]{2,1,0:T(2,128)(2,1)}), bf16[8,2,67584]{2,1,0:T(2,128)(2,1)S(1)}, u32[]{:S(2)}, u32[]{:S(2)}) async-start(bf16[8,2,67584]{2,1,0:T(2,128)(2,1)} %reshape.620), calls=%async_computation.1 | async-start | bytes 4325376 | tf_op jit(solution)/shard_map/all_to_all | solution.py:105
  1228.6 26.0 %copy-start.4 = (s32[4096]{0:T(1024)S(1)}, s32[4096]{0:T(1024)}, u32[]{:S(2)}) copy-start(s32[4096]{0:T(1024)} %get-tuple-element.93) | copy-start | bytes 49156
  1228.6 26.0 %copy-start.6 = (s32[4096]{0:T(1024)S(1)}, s32[4096]{0:T(1024)}, u32[]{:S(2)}) copy-start(s32[4096]{0:T(1024)} %copy-done.5) | copy-start | bytes 49156
  1249.3 31.9 %all-to-all-start.3 = ((bf16[8,2,67584]{2,1,0:T(2,128)(2,1)}), bf16[8,2,67584]{2,1,0:T(2,128)(2,1)}, u32[]{:S(2)}, u32[]{:S(2)}) async-start(bf16[8,2,67584]{2,1,0:T(2,128)(2,1)} %reshape.622), calls=%async_computation.3 | async-start | bytes 4325376 | tf_op jit(solution)/shard_map/all_to_all | solution.py:111
  1420.0 22.0 %copy-start.7 = (pred[4096]{0:T(1024)(128)(4,1)S(1)}, pred[4096]{0:T(1024)(128)(4,1)}, u32[]{:S(2)}) copy-start(pred[4096]{0:T(1024)(128)(4,1)} %get-tuple-element.92) | copy-start | bytes 12292
  1420.0 22.0 %copy-start.8 = (pred[4096]{0:T(1024)(128)(4,1)S(1)}, pred[4096]{0:T(1024)(128)(4,1)}, u32[]{:S(2)}) copy-start(pred[4096]{0:T(1024)(128)(4,1)} %get-tuple-element.108) | copy-start | bytes 12292
  1442.0 10.0 copy-start.2
  1442.0 10.0 copy-start.9
  1617.2 9.8 copy-start.3
  1617.2 14.6 slice-start.2
  1617.2 15.5 slice-start.3
  1627.0 6.2 slice-start.4
Sparse Core Ops, SparseCore 0:
  48.6 289.8 all-reduce.10
  492.8 597.8 all-reduce.6
  1141.7 475.4 all-reduce.8
where the time goes:
time: 1650 us; the launch traced here: 1640 us
  waiting for transfers between devices  796 us (48%)
  matrix products  348 us (21%)
  local copies, waits for them, and re-layouts  322 us (20%)
  other arithmetic  144 us (9%)
  starting transfers between devices  19.4 us (1%)
    psum x1, waiting for transfers between devices, body(): part_w1, part_w3, part_w2 = lax.psum((part_w1, part_w3, part_w2), 'expert')  462 us
    psum x1, waiting for transfers between devices, body(): grad_w1, grad_w3, grad_w2 = lax.psum((grad_w1, grad_w3, grad_w2), 'data')  157 us
    psum x1, waiting for transfers between devices, body(): lax.psum((owned_copy(w_in1), owned_copy(w_in3), owned_copy(w_out)), 'expe...  130 us
    dot_general x2, matrix products, expert_bwd(): jnp.einsum('esd,efd->esf', do_rows, w_c, preferred_element_type=jnp.float32)  66.2 us
    unnamed x50, local copies, waits for them, and re-layouts  47.7 us
    gather x2, local copies, waits for them, and re-layouts, combine(): jnp.take(hot_vals, hot_rows, axis=0, mode='fill', fill_value=0)  44 us
    dot_general x2, matrix products, expert_bwd(): jnp.einsum('esd,esf->edf', x_rows, d_pre_b, preferred_element_type=jnp.fl...  40 us
    dot_general x2, matrix products, expert_bwd(): jnp.einsum('esf,esd->efd', hidden, do_rows, preferred_element_type=jnp.fl...  39.7 us
  transfers between devices with their start and end apart: 7, of which 6 were waited for; matrix products, arithmetic and copies ran while one was open for 33% of the time, Pallas kernels for 0%

commit v1 on v0

v1 whole, which is shorter than its diff:
```python
import functools

import jax
import jax.numpy as jnp
from jax import lax
from jax.experimental import pallas as pl
from jax.experimental.pallas import tpu as pltpu
from jax.sharding import PartitionSpec as P

N_HOT = 2
TILE = 16
BLOCK = 256
VMEM_LIMIT = 66_000_000
MESH = pl.DeviceIdType.MESH
ANY = pl.BlockSpec(memory_space=pl.ANY)
bf16, f32, i32 = jnp.bfloat16, jnp.float32, jnp.int32


def capacities(tok_dev, n_exp):
    cap_hot = 3 * tok_dev // 8
    cap_cold = max(8, ((tok_dev - N_HOT * cap_hot) // (n_exp - N_HOT) + 7) // 8 * 8)
    return cap_cold, cap_hot


def dot(a, b, ca, cb):
    return lax.dot_general(a, b, (((ca,), (cb,)), ((), ())), preferred_element_type=f32)


def route_tables(routes, core, n_exp, cap_cold, cap_hot):
    tok = routes.shape[0]
    blocks = tok // BLOCK
    n_seg = N_HOT + n_exp
    flat = routes.reshape(blocks, BLOCK)
    half = n_exp // 2
    mine, other = jnp.where(core == 0, 0, half), jnp.where(core == 0, half, 0)
    seg = jnp.where(flat == mine, 0, jnp.where(flat == other, 1, N_HOT + flat))
    count = jnp.sum((seg[:, :, None] == jnp.arange(n_seg)[None, None, :]).astype(i32), axis=1)
    before = jnp.arange(blocks)[:, None] > jnp.arange(blocks)[None, :]
    base = jnp.sum(jnp.where(before[:, :, None], count[None], 0), axis=1)
    cap = jnp.where(jnp.arange(n_seg) < N_HOT, cap_hot, cap_cold)[None, :]
    kept = jnp.clip(cap - base, 0, count)
    tiles = jnp.where(kept > 0, (base % TILE + kept + TILE - 1) // TILE, 0)
    lower = jnp.arange(n_seg)[:, None] < jnp.arange(n_seg)[None, :]
    first = jnp.sum(jnp.where(lower[None], tiles[:, :, None], 0), axis=1)
    offset = jnp.where(jnp.arange(n_seg) < N_HOT, 0, (jnp.arange(n_seg) - N_HOT) * cap_cold)[None, :]
    dest = (offset + jnp.minimum(base, cap)) // TILE
    row = (TILE * first + base % TILE).astype(f32)
    limit = (cap - base).astype(f32)
    return seg, first, tiles, dest, row, limit


def dispatch_kernel(first_ref, tiles_ref, dest_ref, seg_ref, row_ref, x_ref, dy_ref, gate_ref,
                    mine_ref, other_ref, cold_ref, stage, *, n_seg):
    j = pl.program_id(0)

    @pl.when(j == 0)
    def _():
        for ref in (mine_ref, other_ref, cold_ref):
            @pl.loop(0, ref.shape[0] // TILE)
            def _(i):
                ref[pl.ds(pl.multiple_of(i * TILE, TILE), TILE), :] = jnp.zeros((TILE, ref.shape[1]), bf16)

    seg = seg_ref[0]
    hit = lax.broadcasted_iota(i32, (n_seg, BLOCK), 0) == seg
    upto = lax.broadcasted_iota(i32, (BLOCK, BLOCK), 0) <= lax.broadcasted_iota(i32, (BLOCK, BLOCK), 1)
    rank = dot(hit.astype(f32).astype(bf16), upto.astype(f32).astype(bf16), 1, 0)
    row, limit = row_ref[0, :, 0:1], row_ref[0, :, 1:2]
    slot = jnp.sum(jnp.where(hit & (rank <= limit), rank + row, 0.0), axis=0, keepdims=True) - 1.0
    pick = (lax.broadcasted_iota(i32, (2 * BLOCK, BLOCK), 0).astype(f32) == slot).astype(f32).astype(bf16)
    d = x_ref.shape[1]
    do = (dy_ref[...].astype(f32) * gate_ref[...]).astype(bf16)
    stage[:, :d] = dot(pick, x_ref[...], 1, 0).astype(bf16)
    stage[:, d:] = dot(pick, do, 1, 0).astype(bf16)
    for s in range(n_seg):
        ref = (mine_ref, other_ref)[s] if s < N_HOT else cold_ref
        a0, t0 = first_ref[j, s], dest_ref[j, s]

        @pl.loop(0, tiles_ref[j, s])
        def _(i):
            src = pl.ds(pl.multiple_of((a0 + i) * TILE, TILE), TILE)
            dst = pl.ds(pl.multiple_of((t0 + i) * TILE, TILE), TILE)
            ref[dst, :] = ref[dst, :] + stage[src, :]


def dispatch(tokens, grad_y, gates, tables, cap_cold, cap_hot, n_exp):
    seg, first, tiles, dest, row, limit = tables
    tok, d = tokens.shape
    blocks, n_seg = first.shape
    whole = lambda n: pl.BlockSpec((n, 2 * d), lambda j, *_: (0, 0), pipeline_mode=pl.Buffered(1))
    rows = pl.BlockSpec((BLOCK, d), lambda j, *_: (j, 0))
    sizes = (cap_hot, cap_hot, n_exp * cap_cold)
    return pl.pallas_call(
        functools.partial(dispatch_kernel, n_seg=n_seg),
        grid_spec=pltpu.PrefetchScalarGridSpec(
            num_scalar_prefetch=3, grid=(blocks,),
            in_specs=[pl.BlockSpec((1, 1, BLOCK), lambda j, *_: (j, 0, 0)),
                      pl.BlockSpec((1, n_seg, 2), lambda j, *_: (j, 0, 0)),
                      rows, rows, pl.BlockSpec((BLOCK, 1), lambda j, *_: (j, 0))],
            out_specs=[whole(n) for n in sizes],
            scratch_shapes=[pltpu.VMEM((2 * BLOCK, 2 * d), bf16)]),
        out_shape=[jax.ShapeDtypeStruct((n, 2 * d), bf16) for n in sizes],
        compiler_params=pltpu.CompilerParams(dimension_semantics=("arbitrary",), vmem_limit_bytes=VMEM_LIMIT),
        cost_estimate=pl.CostEstimate(flops=tok * 2 * BLOCK * 4 * d, bytes_accessed=tok * d * 9, transcendentals=0),
        name="dispatch",
    )(first, tiles, dest, seg[:, None, :], jnp.stack([row, limit], axis=-1), tokens, grad_y, gates)


def combine_kernel(first_ref, tiles_ref, dest_ref, seg_ref, row_ref, gate_ref, mine_ref, other_ref, cold_ref,
                   y_ref, gx_ref, stage, *, n_seg):
    j = pl.program_id(0)

    @pl.when(j == 0)
    def _():
        stage[...] = jnp.zeros_like(stage)

    for s in range(n_seg):
        ref = (mine_ref, other_ref)[s] if s < N_HOT else cold_ref
        a0, t0 = first_ref[j, s], dest_ref[j, s]

        @pl.loop(0, tiles_ref[j, s])
        def _(i):
            src = pl.ds(pl.multiple_of((t0 + i) * TILE, TILE), TILE)
            dst = pl.ds(pl.multiple_of((a0 + i) * TILE, TILE), TILE)
            stage[dst, :] = ref[src, :]

    hit = lax.broadcasted_iota(i32, (BLOCK, n_seg), 1) == seg_ref[...]
    upto = lax.broadcasted_iota(i32, (BLOCK, BLOCK), 1) <= lax.broadcasted_iota(i32, (BLOCK, BLOCK), 0)
    rank = dot(upto.astype(f32).astype(bf16), hit.astype(f32).astype(bf16), 1, 0)
    row, limit = row_ref[0, 0:1, :], row_ref[0, 1:2, :]
    slot = jnp.sum(jnp.where(hit & (rank <= limit), rank + row, 0.0), axis=1, keepdims=True) - 1.0
    pick = (lax.broadcasted_iota(i32, (BLOCK, 2 * BLOCK), 1).astype(f32) == slot).astype(f32).astype(bf16)
    d = y_ref.shape[1]
    y_ref[...] = (dot(pick, stage[:, :d], 1, 0) * gate_ref[...]).astype(bf16)
    gx_ref[...] = dot(pick, stage[:, d:], 1, 0).astype(bf16)


def combine(mine, other, cold, gates, tables):
    seg, first, tiles, dest, row, limit = tables
    blocks, n_seg = first.shape
    d = mine.shape[1] // 2
    tok = blocks * BLOCK
    whole = lambda a: pl.BlockSpec(a.shape, lambda j, *_: (0, 0), pipeline_mode=pl.Buffered(1))
    rows = pl.BlockSpec((BLOCK, d), lambda j, *_: (j, 0))
    column = pl.BlockSpec((BLOCK, 1), lambda j, *_: (j, 0))
    return pl.pallas_call(
        functools.partial(combine_kernel, n_seg=n_seg),
        grid_spec=pltpu.PrefetchScalarGridSpec(
            num_scalar_prefetch=3, grid=(blocks,),
            in_specs=[column, pl.BlockSpec((1, 2, n_seg), lambda j, *_: (j, 0, 0)), column,
                      whole(mine), whole(other), whole(cold)],
            out_specs=[rows, rows],
            scratch_shapes=[pltpu.VMEM((2 * BLOCK, 2 * d), bf16)]),
        out_shape=[jax.ShapeDtypeStruct((tok, d), bf16)] * 2,
        compiler_params=pltpu.CompilerParams(dimension_semantics=("arbitrary",), vmem_limit_bytes=VMEM_LIMIT),
        cost_estimate=pl.CostEstimate(flops=tok * 2 * BLOCK * 4 * d, bytes_accessed=tok * d * 9, transcendentals=0),
        name="combine",
    )(first, tiles, dest, seg.reshape(tok, 1), jnp.stack([row, limit], axis=1), gates, mine, other, cold)


def expert_kernel(*refs, n_src, roles, sizes, tb, sb, fc):
    refs = list(refs)
    srcs = [refs.pop(0) for _ in range(n_src)]
    n_w = len(roles)
    sources = [[refs.pop(0) for _ in range(3)] for _ in range(n_w)]
    outs = [refs.pop(0) for _ in range(n_src)]
    g1_ref, g3_ref, g2_ref = refs[:3]
    xs, xt, dt, acc, g2t, w1b, w3b, w2b, sem_x, sem_w = refs[3:]
    f, t = pl.program_id(0), pl.program_id(1)
    nf, nt = pl.num_programs(0), pl.num_programs(1)
    d = g1_ref.shape[0]

    def weight_copies(source, chunk, slot):
        w1, w3, w2 = source
        at = pl.ds(pl.multiple_of(chunk * fc, fc), fc)
        return [pltpu.make_async_copy(w1.at[:, at], w1b.at[slot], sem_w.at[slot, 0]),
                pltpu.make_async_copy(w3.at[:, at], w3b.at[slot], sem_w.at[slot, 1]),
                pltpu.make_async_copy(w2.at[at, :], w2b.at[slot], sem_w.at[slot, 2])]

    def fetch(chunk, slot):
        for pred, source in zip(roles, sources):
            def go(source=source):
                for c in weight_copies(source, chunk, slot):
                    c.start()
            if pred is None:
                go()
            else:
                pl.when(pred())(go)

    @pl.when(jnp.logical_and(f == 0, t == 0))
    def _():
        fetch(0, 0)
        copies, at = [], 0
        for i, src in enumerate(srcs):
            copies.append(pltpu.make_async_copy(src, xs.at[pl.ds(at, sizes[i]), :], sem_x.at[i]))
            at += sizes[i]
        for c in copies:
            c.start()
        for c in copies:
            c.wait()

    slot = lax.rem(f, 2)

    @pl.when(t == 0)
    def _():
        for c in weight_copies(sources[0], f, slot):
            c.wait()

        @pl.when(f + 1 < nf)
        def _():
            fetch(f + 1, 1 - slot)

        g1_ref[...] = jnp.zeros_like(g1_ref)
        g3_ref[...] = jnp.zeros_like(g3_ref)
        g2t[...] = jnp.zeros_like(g2t)

    rows = pl.ds(pl.multiple_of(t * tb, tb), tb)

    @pl.when(f == 0)
    def _():
        xt[t] = xs[rows, :d].T
        dt[t] = xs[rows, d:].T
        acc[rows, :] = jnp.zeros((tb, 2 * d), f32)

    w1, w3, w2 = w1b[slot], w3b[slot], w2b[slot]
    hs, das, dbs = [], [], []
    for i in range(tb // sb):
        part = pl.ds(pl.multiple_of(t * tb + i * sb, sb), sb)
        x, do = xs[part, :d], xs[part, d:]
        a = dot(x, w1, 1, 0).astype(bf16).astype(f32)
        b = dot(x, w3, 1, 0).astype(bf16).astype(f32)
        dh = dot(do, w2, 1, 1)
        sg = jax.nn.sigmoid(a)
        h = (a * sg * b).astype(bf16)
        db = (dh * a * sg).astype(bf16)
        da = (dh * b * sg * (1.0 + a * (1.0 - sg))).astype(bf16)
        hs.append(h), das.append(da), dbs.append(db)
        acc[part, :d] += dot(h, w2, 1, 0)
        acc[part, d:] += dot(da, w1, 1, 1) + dot(db, w3, 1, 1)
    h, da, db = jnp.concatenate(hs), jnp.concatenate(das), jnp.concatenate(dbs)
    xT, dT = xt[t], dt[t]
    g1_ref[...] += dot(xT, da, 1, 0)
    g3_ref[...] += dot(xT, db, 1, 0)
    g2t[...] += dot(dT, h, 1, 0)

    @pl.when(t == nt - 1)
    def _():
        g2_ref[...] = g2t[...].T

    at = 0
    for i, out in enumerate(outs):
        n = sizes[i] // tb

        @pl.when(jnp.logical_and(f == nf - 1, jnp.logical_and(t >= at, t < at + n)))
        def _():
            out[...] = acc[rows, :].astype(bf16)
        at += n


def expert_pass(srcs, weights, roles, tb, sb, fc, name):
    d, ff = weights[0][0].shape
    sizes = [s.shape[0] for s in srcs]
    total = sum(sizes)
    nf, nt = ff // fc, total // tb
    specs, at = [], 0
    for n in sizes:
        n_b = n // tb

        def index(f, t, at=at, n_b=n_b):
            return jnp.where(f == nf - 1, jnp.clip(t - at, 0, n_b - 1), 0), 0
        specs.append(pl.BlockSpec((tb, 2 * d), index))
        at += n_b
    column = pl.BlockSpec((d, fc), lambda f, t: (0, f))
    res = pl.pallas_call(
        functools.partial(expert_kernel, n_src=len(srcs), roles=roles, sizes=sizes, tb=tb, sb=sb, fc=fc),
        grid=(nf, nt),
        in_specs=[ANY] * (len(srcs) + 3 * len(weights)),
        out_specs=specs + [column, column, pl.BlockSpec((fc, d), lambda f, t: (f, 0))],
        out_shape=[jax.ShapeDtypeStruct(s.shape, bf16) for s in srcs] + [
            jax.ShapeDtypeStruct((d, ff), f32)] * 2 + [jax.ShapeDtypeStruct((ff, d), f32)],
        scratch_shapes=[pltpu.VMEM((total, 2 * d), bf16), pltpu.VMEM((nt, d, tb), bf16), pltpu.VMEM((nt, d, tb), bf16),
                        pltpu.VMEM((total, 2 * d), f32), pltpu.VMEM((d, fc), f32),
                        pltpu.VMEM((2, d, fc), bf16), pltpu.VMEM((2, d, fc), bf16), pltpu.VMEM((2, fc, d), bf16),
                        pltpu.SemaphoreType.DMA((len(srcs),)), pltpu.SemaphoreType.DMA((2, 3))],
        compiler_params=pltpu.CompilerParams(
            dimension_semantics=("arbitrary", "arbitrary"), vmem_limit_bytes=VMEM_LIMIT),
        cost_estimate=pl.CostEstimate(flops=total * d * ff * 18, bytes_accessed=d * ff * 18 + total * d * 8,
                                      transcendentals=total * ff),
        name=name,
    )(*srcs, *[w for group in weights for w in group])
    return res[:len(srcs)], res[len(srcs):]


def gradient_kernel(*refs, nx, ny, lag):
    g, c, o = refs[0:3], refs[3:6], refs[6:9]
    (xsa, xsb, xfa, xfb, la, lb, yha, yhb, yfa, yfb, aga, agb,
     s_xs, s_xr, s_loc, s_agl, s_own, s_ags, s_agr, s_rs, s_rr, s_hs, s_hr, s_fs, s_fr, s_gs, s_gr) = refs[9:]
    q, r = lax.axis_index("data"), lax.axis_index("expert")
    x, core = r // 2, lax.rem(r, 2)
    n_dev = 2 * nx
    owner = jnp.where(core == 0, 0, n_dev // 2)
    is_hot = jnp.logical_or(r == 0, r == n_dev // 2)
    unit = [ref.shape[0] // (nx * ny) for ref in g]
    kinds = range(3)

    def pick(a, b, kind, *lead):
        return a.at[(*lead, kind)] if kind < 2 else b.at[lead]

    def rows(kind, j, i, lo=0, n=None):
        u = unit[kind]
        start = pl.multiple_of((lax.rem(j + 4 * ny, ny) * nx + lax.rem(i + 4 * nx, nx)) * u + lo, 8)
        return pl.ds(start, u if n is None else n)

    def half(kind, which):
        h = unit[kind] // 2
        return pl.ds(which * h, h)

    def remote(src, dst, send, recv, **where):
        return pltpu.make_async_remote_copy(src_ref=src, dst_ref=dst, send_sem=send, recv_sem=recv,
                                            device_id=where, device_id_type=MESH)

    def add(dst, a, b, n, step):
        @pl.loop(0, n // step)
        def _(i):
            at = pl.ds(pl.multiple_of(i * step, 8), step)
            dst[at, :] = a[at, :] + b[at, :]

    step_rows = [8, 8, 32]
    east = lambda d: lax.rem(r + (2 if d == 0 else n_dev - 2), n_dev)
    north = lambda d: lax.rem(q + (1 if d == 0 else ny - 1), ny)
    rel_of = ((2, 1), (3, 0))

    def chunk(d, s):
        return x - 1 - s if d == 0 else x + 1 + s

    def local(d, s, jj, kind):
        return pltpu.make_async_copy(g[kind].at[rows(kind, q + rel_of[d][jj], chunk(d, s)), :],
                                     pick(la, lb, kind, d), s_loc.at[d, kind])

    def x_send(d, s, jj, kind):
        k = jj * 3 + kind
        src = (g[kind].at[rows(kind, q + rel_of[d][jj], chunk(d, 0)), :] if s == 0
               else pick(xsa, xsb, kind, d, s - 1, jj))
        return remote(src, pick(xsa, xsb, kind, d, s, jj), s_xs.at[d, s, k], s_xr.at[d, s, k], expert=east(d))

    def ag_load(kind, i):
        u = unit[kind]
        return pltpu.make_async_copy(c[kind].at[pl.ds(i * u, u), :], pick(aga, agb, kind, i), s_agl.at[kind, i])

    def ag_own(kind, i):
        return pltpu.make_async_copy(pick(aga, agb, kind, i), o[kind].at[rows(kind, q, i), :], s_own.at[kind, i])

    def ag_send(d, kind, i):
        return remote(pick(aga, agb, kind, i), o[kind].at[rows(kind, q, i), :],
                      s_ags.at[d, kind, i], s_agr.at[d, kind, i], data=north(d))

    def ag_relay(d, kind, i):
        h = unit[kind] // 2
        from_q = q - 1 if d == 0 else q + 1
        at = rows(kind, from_q, i, d * h, h)
        return remote(o[kind].at[at, :], o[kind].at[at, :], s_rs.at[d, kind, i], s_rr.at[d, kind, i], data=north(d))

    def gather_send(kind):
        return remote(pick(xfa, xfb, kind, 0), aga.at[x, kind] if kind < 2 else agb.at[x],
                      s_gs.at[kind], s_gr.at[kind, x], expert=owner)

    def y_half(d, kind):
        return remote(pick(xfa, xfb, kind, 2).at[half(kind, d), :], pick(yha, yhb, kind, d),
                      s_hs.at[d, kind], s_hr.at[d, kind], data=north(d))

    def y_full(d, kind):
        return remote(pick(xfa, xfb, kind, 1 if d == 0 else 3), pick(yfa, yfb, kind, d),
                      s_fs.at[d, kind], s_fr.at[d, kind], data=north(d))

    def ag_start(kind, i):
        ag_own(kind, i).start()
        for d in range(2):
            ag_send(d, kind, i).start()

    def ag_pass_on(kind, i):
        for d in range(2):
            ag_send(d, kind, i).wait_recv()
            ag_relay(d, kind, i).start()

    items = [(kind, i) for i in range(nx) for kind in kinds]

    order = {(d, kind): [] for d in range(2) for kind in kinds}
    rounds = []
    for n in range(6 + 3 * lag):
        now = []
        for s in (3, 2, 1, 0):
            k = n - lag * s
            if 0 <= k < 6:
                now.append((s, k // 3, k % 3))
        rounds.append(now)
        for s, jj, kind in now:
            if s > 0:
                for d in range(2):
                    order[d, kind].append((s, jj))

    position = {key: 0 for key in order}
    for d in range(2):
        for kind in kinds:
            s, jj = order[d, kind][0]
            local(d, s, jj, kind).start()

    @pl.when(jnp.logical_not(is_hot))
    def _():
        for kind, i in items:
            ag_load(kind, i).start()

    passed = 0
    for n, now in enumerate(rounds):
        for s, jj, kind in now:
            for d in range(2):
                if s == 0:
                    x_send(d, 0, jj, kind).start()
                    continue
                x_send(d, s - 1, jj, kind).wait_recv()
                local(d, s, jj, kind).wait()
                slot = pick(xsa, xsb, kind, d, s - 1, jj)
                dst = slot if s < 3 else pick(xfa, xfb, kind, rel_of[d][jj])
                add(dst, slot, pick(la, lb, kind, d), unit[kind], step_rows[kind])
                if s < 3:
                    x_send(d, s, jj, kind).start()
                position[d, kind] += 1
                if position[d, kind] < len(order[d, kind]):
                    s2, jj2 = order[d, kind][position[d, kind]]
                    local(d, s2, jj2, kind).start()
            if s == 3 and jj == 0:
                for d in range(2):
                    y_half(d, kind).start()
            if s == 3 and jj == 1:
                for d in range(2):
                    y_half(d, kind).wait_recv()
                    piece = pick(xfa, xfb, kind, 1 if d == 0 else 3).at[half(kind, d), :]
                    add(piece, piece, pick(yha, yhb, kind, d), unit[kind] // 2, 8)
                    y_full(d, kind).start()

        @pl.when(jnp.logical_not(is_hot))
        def _():
            if n == 0:
                for kind, i in items:
                    ag_load(kind, i).wait()
                    ag_start(kind, i)
            elif n <= len(items):
                ag_pass_on(*items[n - 1])
        passed = min(n, len(items))

    @pl.when(jnp.logical_not(is_hot))
    def _():
        for kind, i in items[passed:]:
            ag_pass_on(kind, i)

    for kind in kinds:
        for d in range(2):
            y_full(d, kind).wait_recv()
        piece = pick(xfa, xfb, kind, 0)
        add(piece, piece, pick(yfa, yfb, kind, 0), unit[kind], step_rows[kind])
        mine = r == owner

        @pl.when(mine)
        def _():
            add(pick(aga, agb, kind, 0), piece, pick(yfa, yfb, kind, 1), unit[kind], step_rows[kind])

        @pl.when(jnp.logical_not(mine))
        def _():
            add(piece, piece, pick(yfa, yfb, kind, 1), unit[kind], step_rows[kind])
            gather_send(kind).start()

    @pl.when(is_hot)
    def _():
        for kind in kinds:
            for i in range(nx):
                if i == 0:
                    @pl.when(r != 0)
                    def _():
                        pltpu.make_async_remote_copy(
                            src_ref=pick(xfa, xfb, kind, 0), dst_ref=pick(aga, agb, kind, i), send_sem=s_gs.at[kind],
                            recv_sem=s_gr.at[kind, i], device_id={"expert": owner}, device_id_type=MESH).wait_recv()
                else:
                    pltpu.make_async_remote_copy(
                        src_ref=pick(xfa, xfb, kind, 0), dst_ref=pick(aga, agb, kind, i), send_sem=s_gs.at[kind],
                        recv_sem=s_gr.at[kind, i], device_id={"expert": owner}, device_id_type=MESH).wait_recv()
                ag_start(kind, i)
        for kind in kinds:
            for i in range(nx):
                ag_pass_on(kind, i)

    for d in range(2):
        for kind in kinds:
            for jj in range(2):
                for s in range(3):
                    x_send(d, s, jj, kind).wait_send()
            y_half(d, kind).wait_send()
            y_full(d, kind).wait_send()
            for i in range(nx):
                ag_send(d, kind, i).wait_send()
                ag_relay(d, kind, i).wait()
    for kind in kinds:
        for i in range(nx):
            ag_own(kind, i).wait()

        @pl.when(r != owner)
        def _():
            gather_send(kind).wait_send()


def finish_gradients(hot, cold, nx, ny, lag=2):
    ua, ub = hot[0].shape[0] // (nx * ny), hot[2].shape[0] // (nx * ny)
    wa, wb = hot[0].shape[1], hot[2].shape[1]
    va = lambda *lead: pltpu.VMEM((*lead, 2, ua, wa), f32)
    vb = lambda *lead: pltpu.VMEM((*lead, ub, wb), f32)
    sem = lambda *n: pltpu.SemaphoreType.DMA(n)
    sent = sum(h.size * 4 for h in hot)
    return pl.pallas_call(
        functools.partial(gradient_kernel, nx=nx, ny=ny, lag=lag),
        in_specs=[ANY] * 6, out_specs=[ANY] * 3,
        out_shape=[jax.ShapeDtypeStruct(h.shape, f32) for h in hot],
        scratch_shapes=[
            va(2, 3, 2), vb(2, 3, 2), va(4), vb(4), va(2), vb(2),
            pltpu.VMEM((2, 2, ua // 2, wa), f32), pltpu.VMEM((2, ub // 2, wb), f32), va(2), vb(2),
            va(nx), vb(nx),
            sem(2, 3, 6), sem(2, 3, 6), sem(2, 3), sem(3, nx), sem(3, nx), sem(2, 3, nx), sem(2, 3, nx), sem(2, 3, nx),
            sem(2, 3, nx), sem(2, 3), sem(2, 3), sem(2, 3), sem(2, 3), sem(3), sem(3, nx)],
        compiler_params=pltpu.CompilerParams(has_side_effects=True, vmem_limit_bytes=VMEM_LIMIT),
        cost_estimate=pl.CostEstimate(flops=sent, bytes_accessed=4 * sent, transcendentals=0),
        name="finish_gradients",
    )(*hot, *cold)


def solution(mesh):
    n_dev, ny = mesh.shape["expert"], mesh.shape["data"]
    nx = n_dev // 2
    assert nx == 4 and ny == 4
    row_spec = P(("pod", "data", "expert"), None)
    w_spec = P("expert", None, None)
    grad_spec = P(("pod", "expert"), None, None)
    h0, h1 = 0, n_dev // 2

    def body(tokens, routes, gates, grad_y, w_in1, w_in3, w_out):
        tok, d = tokens.shape
        ff = w_in1.shape[2]
        n_exp = w_in1.shape[0] * n_dev
        r = lax.axis_index("expert")
        cap_cold, cap_hot = capacities(tok, n_exp)
        own = (w_in1[0], w_in3[0], w_out[0])

        send = lambda ws, pairs: [lax.ppermute(w, "expert", pairs) for w in ws]
        p1 = send(own, [(h0, h0 + 2), (h1, h1 + 3)])
        p2 = send(own, [(h0, n_dev - 2), (h1, h1 - 1)])
        p0 = send(own, [(h1, h1 + 1)])
        p3 = send((p1[0], p1[2]), [(h0 + 2, h1), (h1 + 3, h0 + 1)])
        p4 = send((p2[1],), [(n_dev - 2, h1), (h1 - 1, h0 + 1)])
        hot_w = [own, p0, p1, p2, (p3[0], p4[0], p3[1])]

        def role(*members):
            def test():
                me = lax.axis_index("expert")
                hit = me == members[0]
                for m in members[1:]:
                    hit = jnp.logical_or(hit, me == m)
                return hit
            return test
        roles = [role(h0), role(h1 + 1), role(h0 + 2, h1 + 3), role(n_dev - 2, h1 - 1), role(h1, h0 + 1)]

        tables = route_tables(routes, lax.rem(r, 2), n_exp, cap_cold, cap_hot)
        mine, other, cold = dispatch(tokens, grad_y, gates, tables, cap_cold, cap_hot, n_exp)
        swap = [(i, i ^ 1) for i in range(n_dev)]
        guest = lax.ppermute(other, "expert", swap)
        a2a = lambda v: lax.all_to_all(v.reshape(n_dev, cap_cold, 2 * d), "expert", 0, 0, tiled=True).reshape(v.shape)
        recv = a2a(cold)

        (cold_out,), cold_g = expert_pass([recv], [own], [None], recv.shape[0], recv.shape[0] // 2, 512, "cold")
        part = [lax.psum_scatter(v, "data", scatter_dimension=0, tiled=True) for v in cold_g]
        back = a2a(cold_out)
        (mine_out, guest_out), hot_g = expert_pass([mine, guest], hot_w, roles, 512, 512, 512, "hot")
        other_out = lax.ppermute(guest_out, "expert", swap)
        grads = finish_gradients(hot_g, part, nx, ny)
        y, gx = combine(mine_out, other_out, back, gates, tables)
        return (y, gx, *[v[None] for v in grads])

    return jax.shard_map(body, mesh=mesh,
                         in_specs=(row_spec, row_spec, row_spec, row_spec, w_spec, w_spec, w_spec),
                         out_specs=(row_spec, row_spec, grad_spec, grad_spec, grad_spec),
                         check_vma=False)
```

time: 1650 us -> 1050 us (0.64)
  the two profiles are of different devices: /device:TPU:97 before, /device:TPU:96 now
where the time goes in v1:
time: 1050 us
  Pallas kernels  678 us (65%)
  waiting for transfers between devices  218 us (21%)
  starting transfers between devices  55.4 us (5%)
  blocking collectives  55.3 us (5%)
  local copies, waits for them, and re-layouts  25.2 us (2%)
  between operations  14.1 us (1%)
    pallas_call x1, Pallas kernels, finish_gradients(): pl.pallas_call(functools.partial(gradient_kernel, nx=nx, ny=ny, lag=lag),...  378 us
    pallas_call x2, Pallas kernels, expert_pass(): pl.pallas_call(functools.partial(expert_kernel, n_src=len(srcs), roles=ro...  248 us
    ppermute x12, waiting for transfers between devices, body(): send = lambda ws, pairs: [lax.ppermute(w, 'expert', pairs) for w in ws]  167 us
    all_to_all x1, blocking collectives, body(): lax.all_to_all(v.reshape(n_dev, cap_cold, 2 * d), 'expert', 0, 0, tiled=T...  55.3 us
    all_to_all x1, waiting for transfers between devices, body(): lax.all_to_all(v.reshape(n_dev, cap_cold, 2 * d), 'expert', 0, 0, tiled=T...  50.2 us
    ppermute x12, starting transfers between devices, body(): send = lambda ws, pairs: [lax.ppermute(w, 'expert', pairs) for w in ws]  41.4 us
    pallas_call x1, Pallas kernels, dispatch(): pl.pallas_call(functools.partial(dispatch_kernel, n_seg=n_seg), grid_spec...  26.8 us
    pallas_call x1, Pallas kernels, combine(): pl.pallas_call(functools.partial(combine_kernel, n_seg=n_seg), grid_spec=...  24.9 us
  transfers between devices with their start and end apart: 18, of which 6 were waited for; matrix products, arithmetic and copies ran while one was open for 0% of the time, Pallas kernels for 18%

profile of v1, /device:TPU:96, one launch (start us, length us, event | category | flops | bytes accessed | tf_op | source)
XLA Modules:
  0.0 1050.7 jit_solution(14803644806087823029)
XLA Ops:
  7.2 0.1 reduce-scatter.4.cloned.1.call-start
  7.3 0.7 broadcast_add_fusion
  8.1 0.8 broadcast_compare_fusion
  8.8 0.8 copy.51
  9.7 0.8 copy.53
  10.5 0.6 copy.52
  11.2 1.9 fusion.15
  13.0 0.2 convert_reduce_fusion
  13.3 0.1 copy.55
  13.4 0.3 select_reduce_fusion.1
  13.6 0.1 copy.54
  13.7 0.6 add_select_fusion.1
  14.3 0.1 copy.59
  14.4 0.1 select_reduce_fusion.first_ref
  14.6 0.9 copy.64.row_ref
  15.4 2.0 copy.66.gate_ref
  17.4 26.8 %dispatch.1 = (bf16[1536,1536]{1,0:T(8,128)(2,1)}, bf16[1536,1536]{1,0:T(8,128)(2,1)}, bf16[1408,1536]{1,0:T(8,128)(2,1)}) custom-call(s32[16,10]{1,0:T(8,128)} %copy-done.3, s32[16,10]{1,0:T(8,128)} %copy-done.6, s32[16,10]{1,0:T(8,128)} %get-tuple-element.43.dest_ref, s32[16,1,256]{2,1,0:T(1,128)} %bitcast.31, f32[16,10,2]{2,1,0:T(8,128)} %copy.64.row_ref, ...), custom_call_target="tpu_custom_call" | custom-call | flops 6442450944 | bytes 28311552 | tf_op jit(solution)/shard_map/dispatch/pallas_call | solution.py:92
  44.2 55.3 %all_to_all.10 = bf16[8,176,1536]{2,1,0:T(8,128)(2,1)} all-to-all(bf16[8,176,1536]{2,1,0:T(8,128)(2,1)} %bitcast.28), channel_id=1, replica_groups=mesh['pod'=1,'data'=4,'expert'=8] {'expert'}, dimensions={0} | all-to-all | bytes 8650752 | tf_op jit(solution)/shard_map/all_to_all | solution.py:570
  99.5 79.1 %cold.1 = (bf16[1408,1536]{1,0:T(8,128)(2,1)}, f32[768,3072]{1,0:T(8,128)}, f32[768,3072]{1,0:T(8,128)}, f32[3072,768]{1,0:T(8,128)}) custom-call(bf16[1408,1536]{1,0:T(8,128)(2,1)} %bitcast.29, bf16[768,3072]{1,0:T(8,128)(2,1)} %bitcast.33, bf16[768,3072]{1,0:T(8,128)(2,1)} %bitcast.38, bf16[3072,768]{1,0:T(8,128)(2,1)} %bitcast.43), custom_call_target="tpu_custom_call" | custom-call | flops 59793997824 | bytes 51118080 | tf_op jit(solution)/shard_map/cold/pallas_call | solution.py:273
  178.6 0.1 reduce-scatter.4.cloned.1.call-update
  178.7 0.1 reduce-scatter.6.cloned.1.call-start
  178.7 0.7 reduce-scatter.6.cloned.1.call-update
  179.5 0.1 reduce-scatter.8.cloned.1.call-start
  179.5 0.1 collective-permute-start
  179.7 4.7 collective-permute-start.4
  184.3 3.4 collective-permute-start.8
  187.8 3.4 collective-permute-start.6
  191.2 2.8 collective-permute-start.1
  194.0 0.0 collective-permute-done.refs_1_
  194.0 2.9 collective-permute-start.2
  196.9 36.9 %collective-permute-done.4.refs_8_ = bf16[768,3072]{1,0:T(8,128)(2,1)} collective-permute-done((bf16[768,3072]{1,0:T(8,128)(2,1)}, bf16[768,3072]{1,0:T(8,128)(2,1)}, u32[]{:S(2)}, u32[]{:S(2)}) %collective-permute-start.4) | collective-permute-done | bytes 4718624 | tf_op jit(solution)/shard_map/ppermute | solution.py:548
  233.8 2.7 collective-permute-start.3
  236.5 0.7 collective-permute-done.8.refs_12_
  237.2 5.9 collective-permute-start.5
  243.1 41.2 %collective-permute-done.6.refs_10_ = bf16[3072,768]{1,0:T(8,128)(2,1)} collective-permute-done((bf16[3072,768]{1,0:T(8,128)(2,1)}, bf16[3072,768]{1,0:T(8,128)(2,1)}, u32[]{:S(2)}, u32[]{:S(2)}) %collective-permute-start.6) | collective-permute-done | bytes 4718624 | tf_op jit(solution)/shard_map/ppermute | solution.py:548
  284.4 3.4 collective-permute-start.7
  287.8 0.0 collective-permute-done.1.refs_5_
  287.8 3.6 collective-permute-start.9
  291.4 0.0 collective-permute-done.2.refs_6_
  291.4 2.8 collective-permute-start.10
  294.2 0.0 collective-permute-done.3.refs_7_
  294.2 2.9 collective-permute-start.11
  297.1 37.8 %collective-permute-done.5.refs_9_ = bf16[768,3072]{1,0:T(8,128)(2,1)} collective-permute-done((bf16[768,3072]{1,0:T(8,128)(2,1)}, bf16[768,3072]{1,0:T(8,128)(2,1)}, u32[]{:S(2)}, u32[]{:S(2)}) %collective-permute-start.5) | collective-permute-done | bytes 4718624 | tf_op jit(solution)/shard_map/ppermute | solution.py:548
  334.9 2.8 collective-permute-start.12
  337.7 0.1 reduce-scatter.8.cloned.1.call-update
  337.8 0.0 collective-permute-done.7.refs_11_
  337.8 50.0 %collective-permute-done.9.refs_13_ = bf16[3072,768]{1,0:T(8,128)(2,1)} collective-permute-done((bf16[3072,768]{1,0:T(8,128)(2,1)}, bf16[3072,768]{1,0:T(8,128)(2,1)}, u32[]{:S(2)}, u32[]{:S(2)}) %collective-permute-start.9) | collective-permute-done | bytes 4718624 | tf_op jit(solution)/shard_map/ppermute | solution.py:548
  387.8 0.0 collective-permute-done.12.refs_16_
  387.8 168.5 %hot.1 = (bf16[1536,1536]{1,0:T(8,128)(2,1)}, bf16[1536,1536]{1,0:T(8,128)(2,1)}, f32[768,3072]{1,0:T(8,128)}, f32[768,3072]{1,0:T(8,128)}, f32[3072,768]{1,0:T(8,128)}) custom-call(bf16[1536,1536]{1,0:T(8,128)(2,1)} %get-tuple-element.22.refs_0_, bf16[1536,1536]{1,0:T(8,128)(2,1)} %collective-permute-done.refs_1_, bf16[768,3072]{1,0:T(8,128)(2,1)} %bitcast.37, ...), custom_call_target="tpu_custom_call" | custom-call | flops 130459631616 | bytes 61341696 | tf_op jit(solution)/shard_map/hot/pallas_call | solution.py:273
  556.4 9.0 collective-permute-start.13
  565.4 4.7 all-to-all-start.1
  570.2 0.6 pad_maximum_fusion.row_ref
  570.9 50.2 %all-to-all-done.1 = bf16[8,176,1536]{2,1,0:T(8,128)(2,1)} async-done(((bf16[8,176,1536]{2,1,0:T(8,128)(2,1)}), bf16[8,176,1536]{2,1,0:T(8,128)(2,1)}, u32[]{:S(2)}, u32[]{:S(2)}) %all-to-all-start.1) | async-done | bytes 4325408 | tf_op jit(solution)/shard_map/all_to_all | solution.py:570
  621.0 24.9 %combine.1 = (bf16[4096,768]{1,0:T(8,128)(2,1)}, bf16[4096,768]{1,0:T(8,128)(2,1)}) custom-call(s32[16,10]{1,0:T(8,128)} %copy-done.3, s32[16,10]{1,0:T(8,128)} %copy-done.6, s32[16,10]{1,0:T(8,128)} %get-tuple-element.43.dest_ref, s32[4096,1]{1,0:T(8,128)} %get-tuple-element.40.seg_ref, f32[16,2,10]{2,1,0:T(2,128)} %pad_maximum_fusion.row_ref, ...), custom_call_target="tpu_custom_call" | custom-call | flops 6442450944 | bytes 28311552 | tf_op jit(solution)/shard_map/combine/pallas_call | solution.py:145
  646.0 0.0 reduce-scatter.6.cloned.1.call-done.refs_4_
  646.0 0.0 reduce-scatter.8.cloned.1.call-done.refs_5_
  646.0 378.3 %finish_gradients.1 = (f32[768,3072]{1,0:T(8,128)}, f32[768,3072]{1,0:T(8,128)}, f32[3072,768]{1,0:T(8,128)}) custom-call(f32[768,3072]{1,0:T(8,128)} %get-tuple-element.30.refs_0_, f32[768,3072]{1,0:T(8,128)} %get-tuple-element.31.refs_1_, f32[3072,768]{1,0:T(8,128)} %get-tuple-element.32.refs_2_, f32[192,3072]{1,0:T(8,128)} %reduce-scatter.4.cloned.1.call-done.refs_3_, ...), custom_call_target="tpu_custom_call" | custom-call | flops 28311552 | bytes 113246208 | tf_op jit(solution)/shard_map/finish_gradients/pallas_call | solution.py:515
  1024.3 0.0 slice-start
  1024.4 0.0 slice-start.1
  1024.4 9.8 copy.70
  1034.2 4.8 copy.71
  1039.0 0.8 slice-done.1
  1039.8 0.6 slice-done.2
  1040.4 3.7 copy.72
  (35 shorter events, 0.1 us)
Async XLA Ops:
  7.2 8.3 copy-start.7
  7.2 638.8 %reduce-scatter.4.cloned.1.call-start = ((), (), s32[]{:S(2)}) async-start(), calls=%async_computation.5 | async-start | bytes 11796480 | tf_op jit(solution)/shard_map/reduce_scatter | solution.py:574
  7.3 10.1 copy-start.8
  13.0 4.4 copy-start.5
  13.7 0.8 copy-start.1
  14.3 3.1 copy-start.6
  14.5 2.9 copy-start.3
  178.7 467.3 %reduce-scatter.6.cloned.1.call-start = ((), (), s32[]{:S(2)}) async-start(), calls=%async_computation.6 | async-start | bytes 11796480 | tf_op jit(solution)/shard_map/reduce_scatter | solution.py:574
  179.5 466.5 %reduce-scatter.8.cloned.1.call-start = ((), (), s32[]{:S(2)}) async-start(), calls=%async_computation.7 | async-start | bytes 11796480 | tf_op jit(solution)/shard_map/reduce_scatter | solution.py:574
  179.5 14.5 %collective-permute-start = (bf16[1536,1536]{1,0:T(8,128)(2,1)}, bf16[1536,1536]{1,0:T(8,128)(2,1)}, u32[]{:S(2)}, u32[]{:S(2)}) collective-permute-start(bf16[1536,1536]{1,0:T(8,128)(2,1)} %get-tuple-element.23), channel_id=1, source_target_pairs={{0,1},{1,0},{2,3},{3,2},{4,5},{5,4},{6,7},{7,6},{8,9},{9,8},{10,11... | collective-permute-start | bytes 14155784 | tf_op jit(solution)/shard_map/ppermute | solution.py:569
  179.7 54.1 %collective-permute-start.4 = (bf16[768,3072]{1,0:T(8,128)(2,1)}, bf16[768,3072]{1,0:T(8,128)(2,1)}, u32[]{:S(2)}, u32[]{:S(2)}) collective-permute-start(bf16[768,3072]{1,0:T(8,128)(2,1)} %bitcast.34), channel_id=1, source_target_pairs={{0,2},{4,7},{8,10},{12,15},{16,18},{20,23},{24,26},{28,31}} | collective-permute-start | bytes 14155784 | tf_op jit(solution)/shard_map/ppermute | solution.py:548
  184.3 52.9 %collective-permute-start.8 = (bf16[768,3072]{1,0:T(8,128)(2,1)}, bf16[768,3072]{1,0:T(8,128)(2,1)}, u32[]{:S(2)}, u32[]{:S(2)}) collective-permute-start(bf16[768,3072]{1,0:T(8,128)(2,1)} %bitcast.39), channel_id=1, source_target_pairs={{0,6},{4,3},{8,14},{12,11},{16,22},{20,19},{24,30},{28,27}} | collective-permute-start | bytes 14155784 | tf_op jit(solution)/shard_map/ppermute | solution.py:548
  187.8 96.6 %collective-permute-start.6 = (bf16[3072,768]{1,0:T(8,128)(2,1)}, bf16[3072,768]{1,0:T(8,128)(2,1)}, u32[]{:S(2)}, u32[]{:S(2)}) collective-permute-start(bf16[3072,768]{1,0:T(8,128)(2,1)} %bitcast.44), channel_id=1, source_target_pairs={{0,2},{4,7},{8,10},{12,15},{16,18},{20,23},{24,26},{28,31}} | collective-permute-start | bytes 14155784 | tf_op jit(solution)/shard_map/ppermute | solution.py:548
  191.2 96.6 %collective-permute-start.1 = (bf16[768,3072]{1,0:T(8,128)(2,1)}, bf16[768,3072]{1,0:T(8,128)(2,1)}, u32[]{:S(2)}, u32[]{:S(2)}) collective-permute-start(bf16[768,3072]{1,0:T(8,128)(2,1)} %bitcast.35), channel_id=1, source_target_pairs={{4,5},{12,13},{20,21},{28,29}} | collective-permute-start | bytes 14155784 | tf_op jit(solution)/shard_map/ppermute | solution.py:548
  194.0 97.4 %collective-permute-start.2 = (bf16[768,3072]{1,0:T(8,128)(2,1)}, bf16[768,3072]{1,0:T(8,128)(2,1)}, u32[]{:S(2)}, u32[]{:S(2)}) collective-permute-start(bf16[768,3072]{1,0:T(8,128)(2,1)} %bitcast.40), channel_id=1, source_target_pairs={{4,5},{12,13},{20,21},{28,29}} | collective-permute-start | bytes 14155784 | tf_op jit(solution)/shard_map/ppermute | solution.py:548
  233.8 60.4 %collective-permute-start.3 = (bf16[3072,768]{1,0:T(8,128)(2,1)}, bf16[3072,768]{1,0:T(8,128)(2,1)}, u32[]{:S(2)}, u32[]{:S(2)}) collective-permute-start(bf16[3072,768]{1,0:T(8,128)(2,1)} %bitcast.45), channel_id=1, source_target_pairs={{4,5},{12,13},{20,21},{28,29}} | collective-permute-start | bytes 14155784 | tf_op jit(solution)/shard_map/ppermute | solution.py:548
  237.2 97.7 %collective-permute-start.5 = (bf16[768,3072]{1,0:T(8,128)(2,1)}, bf16[768,3072]{1,0:T(8,128)(2,1)}, u32[]{:S(2)}, u32[]{:S(2)}) collective-permute-start(bf16[768,3072]{1,0:T(8,128)(2,1)} %bitcast.41), channel_id=1, source_target_pairs={{0,2},{4,7},{8,10},{12,15},{16,18},{20,23},{24,26},{28,31}} | collective-permute-start | bytes 14155784 | tf_op jit(solution)/shard_map/ppermute | solution.py:548
  284.4 53.4 %collective-permute-start.7 = (bf16[768,3072]{1,0:T(8,128)(2,1)}, bf16[768,3072]{1,0:T(8,128)(2,1)}, u32[]{:S(2)}, u32[]{:S(2)}) collective-permute-start(bf16[768,3072]{1,0:T(8,128)(2,1)} %bitcast.36), channel_id=1, source_target_pairs={{0,6},{4,3},{8,14},{12,11},{16,22},{20,19},{24,30},{28,27}} | collective-permute-start | bytes 14155784 | tf_op jit(solution)/shard_map/ppermute | solution.py:548
  287.8 100.0 %collective-permute-start.9 = (bf16[3072,768]{1,0:T(8,128)(2,1)}, bf16[3072,768]{1,0:T(8,128)(2,1)}, u32[]{:S(2)}, u32[]{:S(2)}) collective-permute-start(bf16[3072,768]{1,0:T(8,128)(2,1)} %bitcast.46), channel_id=1, source_target_pairs={{0,6},{4,3},{8,14},{12,11},{16,22},{20,19},{24,30},{28,27}} | collective-permute-start | bytes 14155784 | tf_op jit(solution)/shard_map/ppermute | solution.py:548
  291.4 96.4 %collective-permute-start.10 = (bf16[768,3072]{1,0:T(8,128)(2,1)}, bf16[768,3072]{1,0:T(8,128)(2,1)}, u32[]{:S(2)}, u32[]{:S(2)}) collective-permute-start(bf16[768,3072]{1,0:T(8,128)(2,1)} %collective-permute-done.4.refs_8_), channel_id=1, source_target_pairs={{2,4},{7,1},{10,12},{15,9},{18,20},{23,17},{26,28},{31,25}} | collective-permute-start | bytes 14155784 | tf_op jit(solution)/shard_map/ppermute | solution.py:548
  294.2 93.6 %collective-permute-start.11 = (bf16[768,3072]{1,0:T(8,128)(2,1)}, bf16[768,3072]{1,0:T(8,128)(2,1)}, u32[]{:S(2)}, u32[]{:S(2)}) collective-permute-start(bf16[768,3072]{1,0:T(8,128)(2,1)} %collective-permute-done.8.refs_12_), channel_id=1, source_target_pairs={{6,4},{3,1},{14,12},{11,9},{22,20},{19,17},{30,28},{27,25}} | collective-permute-start | bytes 14155784 | tf_op jit(solution)/shard_map/ppermute | solution.py:548
  334.9 52.9 %collective-permute-start.12 = (bf16[3072,768]{1,0:T(8,128)(2,1)}, bf16[3072,768]{1,0:T(8,128)(2,1)}, u32[]{:S(2)}, u32[]{:S(2)}) collective-permute-start(bf16[3072,768]{1,0:T(8,128)(2,1)} %collective-permute-done.6.refs_10_), channel_id=1, source_target_pairs={{2,4},{7,1},{10,12},{15,9},{18,20},{23,17},{26,28},{31,25}} | collective-permute-start | bytes 14155784 | tf_op jit(solution)/shard_map/ppermute | solution.py:548
  556.4 13.8 %copy-start.4 = (s32[16,10]{1,0:T(8,128)S(1)}, s32[16,10]{1,0:T(8,128)}, u32[]{:S(2)}) copy-start(s32[16,10]{1,0:T(8,128)} %copy-done.3) | copy-start | bytes 1924
  556.4 13.8 %copy-start.2 = (s32[16,10]{1,0:T(8,128)S(1)}, s32[16,10]{1,0:T(8,128)}, u32[]{:S(2)}) copy-start(s32[16,10]{1,0:T(8,128)} %copy-done.1) | copy-start | bytes 1924
  556.4 13.8 %copy-start.9 = (s32[10]{0:T(128)S(1)}, s32[10]{0:T(128)}, u32[]{:S(2)}) copy-start(s32[10]{0:T(128)} %copy-done.8) | copy-start | bytes 124
  556.4 64.6 %collective-permute-start.13 = (bf16[1536,1536]{1,0:T(8,128)(2,1)}, bf16[1536,1536]{1,0:T(8,128)(2,1)}, u32[]{:S(2)}, u32[]{:S(2)}) collective-permute-start(bf16[1536,1536]{1,0:T(8,128)(2,1)} %get-tuple-element.25), channel_id=1, source_target_pairs={{0,1},{1,0},{2,3},{3,2},{4,5},{5,4},{6,7},{7,6},{8,9},{9,8},{10,11... | collective-permute-start | bytes 14155784 | tf_op jit(solution)/shard_map/ppermute | solution.py:577
  565.4 55.6 %all-to-all-start.1 = ((bf16[8,176,1536]{2,1,0:T(8,128)(2,1)}), bf16[8,176,1536]{2,1,0:T(8,128)(2,1)}, u32[]{:S(2)}, u32[]{:S(2)}) async-start(bf16[8,176,1536]{2,1,0:T(8,128)(2,1)} %bitcast.27), calls=%async_computation.1 | async-start | bytes 8650752 | tf_op jit(solution)/shard_map/all_to_all | solution.py:570
  1024.3 9.8 copy-start
  1024.3 14.6 %slice-start = ((s8[9437184]{0:T(1024)(128)(4,1)}), s8[4194304]{0:T(1024)(128)(4,1)S(1)}, s32[]{:S(2)}) async-start(s8[9437184]{0:T(1024)(128)(4,1)} %bitcast.22), calls=%async_computation.8 | async-start | bytes 8388608
  1024.4 15.4 %slice-start.1 = ((s8[9437184]{0:T(1024)(128)(4,1)}), s8[4194304]{0:T(1024)(128)(4,1)S(1)}, s32[]{:S(2)}) async-start(s8[9437184]{0:T(1024)(128)(4,1)} %bitcast.22), calls=%async_computation.9 | async-start | bytes 8388608
  1034.2 6.2 slice-start.2
Sparse Core Ops, SparseCore 0:
  178.8 87.0 reduce-scatter.3
  268.3 86.1 reduce-scatter.5
  356.9 86.2 reduce-scatter.7
